TPU v7x, 512 devices: a 4x2x32 block of a 4x8x32 slice. The times are simulated.
512 devices in a mesh: rep: 2 (over y), tp: 32 (over z), ep: 8 (over x, core).
Axes of the slice: x: 4, y: 2, z: 32, core: 2. Of those that a mesh axis runs over, the one named last changes fastest.
The devices are a block of a 4x8x32 slice.
Arguments:
- tokens: bfloat16 [1536, 3072], P(('rep', 'ep'), 'tp'), parts along dimension 0, may hold values from -6 to 6
- routing: int32 [1536, 2], P(('rep', 'ep')), parts along dimension 0, may hold values from 0 to 7, all different within a row; in each aligned block of 96 rows (0 to 95, 96 to 191, ...) at most 30 rows name the same one
- route_gates: float32 [1536, 2], P(('rep', 'ep')), parts along dimension 0, may hold values from 0.2 to 1
- expert_gate: bfloat16 [8, 3072, 8192], P('ep', None, 'tp'), may hold values from -0.109375 to 0.109375
- expert_up: bfloat16 [8, 3072, 8192], P('ep', None, 'tp'), may hold values from -0.109375 to 0.109375
- expert_down: bfloat16 [8, 8192, 3072], P('ep', 'tp'), may hold values from -0.0625 to 0.0625
Outputs:
- mixture: bfloat16 [1536, 3072], P(('rep', 'ep'), 'tp'), parts along dimension 0
There are 2 independent parts, one for each index of `rep`. A program takes and returns all parts, laid end to end along the dimension named above; an argument that names none is the same for every part. Nothing has to cross between parts.
Inputs may be any that keep to these rules, and one draw needn't show every extreme that they name: `routing`: each token names two different experts. In each aligned block of 96 tokens (the rows of one index of ep) no expert is named by more than 30 tokens, a bound that some block reaches.
All inputs are finite; a program needn't handle non-finite values.
Results may differ from a plain program's by a relative error of at most 0.0085.
Values may be sent and summed in bfloat16 or wider, within the bound.
No kernel may reach another device: no remote copies, remote signals or barrier semaphores. Data moves between devices by JAX's collectives and lax.ppermute only.
A program may use at most 64 MiB of HBM per device.

v0:
```python
import jax
import jax.numpy as jnp
from jax import lax
from jax.sharding import Mesh
from jax.sharding import PartitionSpec as P

REP_EP = ("rep", "ep")
TP = ("hi", "lo")
BF = jnp.bfloat16
F32 = jnp.float32
LO = 2


def slot_tables(routing, route_gates, experts, rows):
    tok_count, choices_n = routing.shape
    flat_ids = routing.reshape(-1)
    onehot = (flat_ids[:, None] == jnp.arange(experts, dtype=jnp.int32)[None, :]).astype(BF)
    n = tok_count * choices_n
    earlier = (jnp.arange(n)[None, :] < jnp.arange(n)[:, None]).astype(BF)
    before = jnp.dot(earlier, onehot, preferred_element_type=F32)
    position = jnp.sum(before * onehot.astype(F32), axis=1).astype(jnp.int32)
    slot = (flat_ids * rows + position).reshape(tok_count, choices_n)
    picked = slot[:, :, None] == jnp.arange(experts * rows, dtype=jnp.int32)[None, None, :]
    dispatch = picked.astype(F32).sum(axis=1).astype(BF)
    combine = jnp.where(picked, route_gates[:, :, None], 0.0).sum(axis=1)
    return (dispatch, combine)


def body(tokens, routing, route_gates, expert_gate, expert_up, expert_down):
    ep_count = lax.axis_size("ep")
    hi_count = lax.axis_size("hi")
    tok_count, feat = tokens.shape
    capacity = 2 * tok_count // ep_count + tok_count // 16
    rows = -(-capacity // 8) * 8
    slots = ep_count * rows
    wide = hi_count * feat
    hidden_n = expert_gate.shape[2]
    gathered = lax.all_gather(tokens.T, "hi", axis=0, tiled=True)
    dispatch, combine = slot_tables(routing, route_gates, ep_count, rows)
    packed = lax.dot_general(
        dispatch, gathered, (((0,), (1,)), ((), ())), preferred_element_type=F32
    ).astype(BF)
    sent = jnp.broadcast_to(packed.reshape(1, ep_count, rows, wide), (LO, ep_count, rows, wide))
    got = lax.all_to_all(
        sent.reshape(LO * ep_count, rows, wide), ("lo", "ep"), 0, 0, tiled=True
    ).reshape(LO, slots, wide)

    def by_lo(w):
        return (
            w.reshape(hi_count, LO, feat, hidden_n)
            .transpose(1, 0, 2, 3)
            .reshape(LO, wide, hidden_n)
        )

    w_gate, w_up = (by_lo(expert_gate), by_lo(expert_up))
    gate = sum((jnp.dot(got[i], w_gate[i], preferred_element_type=F32) for i in range(LO)))
    up = sum((jnp.dot(got[i], w_up[i], preferred_element_type=F32) for i in range(LO)))
    hidden = (jax.nn.silu(gate) * up).astype(BF)
    w_down = (
        expert_down.reshape(hidden_n, hi_count, LO, feat)
        .transpose(2, 0, 1, 3)
        .reshape(LO, hidden_n, wide)
    )
    part = jnp.stack(
        [jnp.dot(hidden, w_down[i], preferred_element_type=F32).astype(BF) for i in range(LO)]
    )
    back = lax.all_to_all(
        part.reshape(LO * ep_count, rows, wide), ("lo", "ep"), 0, 0, tiled=True
    ).reshape(LO * slots, wide)
    weights = jnp.concatenate([combine] * LO, axis=1).astype(BF)
    mixed = lax.dot_general(
        back, weights, (((0,), (1,)), ((), ())), preferred_element_type=F32
    ).astype(BF)
    shares = lax.all_to_all(mixed.reshape(hi_count, feat, tok_count), "hi", 0, 0, tiled=True)
    return jnp.sum(shares.astype(F32), axis=0).astype(BF).T


def solution(mesh):
    finer = Mesh(
        mesh.devices.reshape(mesh.shape["rep"], mesh.shape["tp"] // LO, LO, mesh.shape["ep"]),
        ("rep", "hi", "lo", "ep"),
    )
    placed = (
        P(REP_EP, TP),
        P(REP_EP, None),
        P(REP_EP, None),
        P("ep", None, TP),
        P("ep", None, TP),
        P("ep", TP, None),
    )
    return jax.shard_map(
        body, mesh=finer, in_specs=placed, out_specs=P(REP_EP, TP), check_vma=False
    )
```

profile of v0, /device:TPU:166, one launch (start us, length us, event | category | flops | bytes accessed | tf_op | source)
XLA Modules:
  0.0 195.5 jit_solution(637232276068174422)
XLA Ops:
  0.0 0.8 copy.28
  0.8 0.1 eq.28
  0.9 0.2 fusion.4
  1.1 0.1 convert_element_type.42
  1.3 0.7 multiply_add_fusion
  2.0 0.8 copy.30
  2.9 68.8 %all_gather.3 = bf16[1536,96]{1,0:T(8,128)(2,1)S(1)} all-gather(bf16[96,96]{1,0:T(8,128)(2,1)S(1)} %bitcast.60), channel_id=1, replica_groups=mesh['rep'=2,'hi'=16,'lo'=2,'ep'=8] {'hi'}, dimensions={0}, use_global_device_ids=true | all-gather | bytes 313344 | tf_op jit(solution)/shard_map/all_gather | solution.py:38
  71.7 0.8 select_reduce_fusion
  72.5 0.4 convolution_convert_fusion.2
  72.9 1.3 broadcast_in_dim.25
  74.2 6.2 %all-to-all-start = ((bf16[16,32,1536]{2,1,0:T(8,128)(2,1)}), bf16[16,32,1536]{2,1,0:T(8,128)(2,1)S(1)}, u32[]{:S(2)}, u32[]{:S(2)}) async-start(bf16[16,32,1536]{2,1,0:T(8,128)(2,1)} %bitcast.2), calls=%async_computation | async-start | bytes 3145728 | tf_op jit(solution)/shard_map/all_to_all | solution.py:44
  80.4 1.7 copy.31
  82.1 2.7 %fusion.13 = (bf16[1,16,96,256]{3,2,0,1:T(8,128)(2,1)}, bf16[1,16,96,256]{3,2,0,1:T(8,128)(2,1)}) fusion(bf16[2,16,96,256]{3,2,0,1:T(8,128)(2,1)} %bitcast.57), kind=kLoop, calls=%fused_computation.27 | loop fusion | bytes 3145728 | tf_op jit(solution)/shard_map/slice | solution.py:56
  84.9 1.3 fusion.14
  86.2 1.3 fusion.12
  87.5 14.4 %all-to-all-done = bf16[16,32,1536]{2,1,0:T(8,128)(2,1)S(1)} async-done(((bf16[16,32,1536]{2,1,0:T(8,128)(2,1)}), bf16[16,32,1536]{2,1,0:T(8,128)(2,1)S(1)}, u32[]{:S(2)}, u32[]{:S(2)}) %all-to-all-start) | async-done | bytes 1572896 | tf_op jit(solution)/shard_map/all_to_all | solution.py:44
  102.0 0.4 fusion.16
  102.4 0.7 copy-done.1
  103.1 0.4 fusion.17
  103.5 0.4 convolution_add_fusion.1
  103.9 0.4 copy-done.6
  104.3 0.4 fusion.3
  104.7 0.4 copy-done.3
  105.0 0.4 fusion
  105.4 0.4 copy-done.2
  105.8 0.4 fusion.1
  106.3 0.1 pad_maximum_fusion
  106.4 24.2 %all_to_all.15 = bf16[16,32,1536]{2,1,0:T(8,128)(2,1)S(1)} all-to-all(bf16[16,32,1536]{2,1,0:T(8,128)(2,1)S(1)} %bitcast.47), channel_id=1, replica_groups=mesh['rep'=2,'hi'=16,'lo'=2,'ep'=8] {'lo','ep'}, dimensions={0} | all-to-all | bytes 3145728 | tf_op jit(solution)/shard_map/all_to_all | solution.py:67
  130.7 0.4 convolution_convert_fusion.3
  131.0 0.3 reshape.60
  131.5 63.3 %all_to_all.16 = bf16[16,96,96]{1,2,0:T(8,128)(2,1)S(1)} all-to-all(bf16[16,96,96]{1,2,0:T(8,128)(2,1)S(1)} %copy.32), channel_id=1, replica_groups=mesh['rep'=2,'hi'=16,'lo'=2,'ep'=8] {'hi'}, dimensions={0} | all-to-all | bytes 589824 | tf_op jit(solution)/shard_map/all_to_all | solution.py:74
  194.8 0.7 reduce_sum.42
  (14 shorter events, 0.3 us)
Async XLA Ops:
  74.2 27.6 %all-to-all-start = ((bf16[16,32,1536]{2,1,0:T(8,128)(2,1)}), bf16[16,32,1536]{2,1,0:T(8,128)(2,1)S(1)}, u32[]{:S(2)}, u32[]{:S(2)}) async-start(bf16[16,32,1536]{2,1,0:T(8,128)(2,1)} %bitcast.2), calls=%async_computation | async-start | bytes 3145728 | tf_op jit(solution)/shard_map/all_to_all | solution.py:44
  82.1 2.8 %copy-start.5 = (bf16[1,3072,256]{2,1,0:T(8,128)(2,1)S(1)}, bf16[1,3072,256]{2,1,0:T(8,128)(2,1)}, u32[]{:S(2)}) copy-start(bf16[1,3072,256]{2,1,0:T(8,128)(2,1)} %param.10) | copy-start | bytes 4718596
  87.5 14.5 %copy-start = (bf16[1,16,96,256]{3,2,0,1:T(8,128)(2,1)S(1)}, bf16[1,16,96,256]{3,2,0,1:T(8,128)(2,1)}, u32[]{:S(2)}) copy-start(bf16[1,16,96,256]{3,2,0,1:T(8,128)(2,1)} %get-tuple-element.10) | copy-start | bytes 2359300
  101.9 1.1 copy-start.1
  102.0 1.5 copy-start.4
  103.1 1.2 copy-start.6
  103.8 1.2 copy-start.3
  104.7 1.2 copy-start.2
where the time goes:
time: 196 us; the launch traced here: 195 us
  blocking collectives  156 us (80%)
  waiting for transfers between devices  14.4 us (7%)
  local copies, waits for them, and re-layouts  12.8 us (7%)
  starting transfers between devices  6.17 us (3%)
  matrix products  3.21 us (2%)
  other arithmetic  2.36 us (1%)
    all_gather x1, blocking collectives, body(): gathered = lax.all_gather(tokens.T, 'hi', axis=0, tiled=True)  68.8 us
    all_to_all x1, blocking collectives, body(): lax.all_to_all(mixed.reshape(hi_count, feat, tok_count), 'hi', 0, 0, tile...  63.3 us
    all_to_all x1, blocking collectives, body(): lax.all_to_all(part.reshape(LO * ep_count, rows, wide), ('lo', 'ep'), 0,...  24.2 us
    all_to_all x1, waiting for transfers between devices, body(): lax.all_to_all(sent.reshape(LO * ep_count, rows, wide), ('lo', 'ep'), 0,...  14.4 us
    all_to_all x1, starting transfers between devices, body(): lax.all_to_all(sent.reshape(LO * ep_count, rows, wide), ('lo', 'ep'), 0,...  6.17 us
    unnamed x17, local copies, waits for them, and re-layouts  5.25 us
  transfers between devices with their start and end apart: 1, of which 1 were waited for; matrix products, arithmetic and copies ran while one was open for 4% of the time, Pallas kernels for 0%

commit v1 on v0

--- a/solution.py
+++ b/solution.py
@@ -35,7 +35,9 @@
     slots = ep_count * rows
     wide = hi_count * feat
     hidden_n = expert_gate.shape[2]
-    gathered = lax.all_gather(tokens.T, "hi", axis=0, tiled=True)
+    gathered = jnp.concatenate(
+        lax.all_to_all(jnp.stack(lax.psum(1, "hi") * [tokens.T]), "hi", 0, 0), axis=0
+    )
     dispatch, combine = slot_tables(routing, route_gates, ep_count, rows)
     packed = lax.dot_general(
         dispatch, gathered, (((0,), (1,)), ((), ())), preferred_element_type=F32

time: 196 us -> 210 us (1.071)
  blocking collectives: 156 us -> 81.9 us
  starting transfers between devices: 6.17 us -> 60.4 us
  waiting for transfers between devices: 14.4 us -> 47.3 us
    all_gather x1 -> x0, blocking collectives: 68.8 us -> none  [body(): gathered = lax.all_gather(tokens.T, 'hi', axis=0, tiled=True)]
    all_to_all x0 -> x1, starting transfers between devices: none -> 42.2 us  [body(): lax.all_to_all(jnp.stack(lax.psum(1, 'hi') * [tokens.T]), 'hi', 0, 0)]
    all_to_all x0 -> x1, waiting for transfers between devices: none -> 33 us  [body(): lax.all_to_all(jnp.stack(lax.psum(1, 'hi') * [tokens.T]), 'hi', 0, 0)]
    all_to_all x1, starting transfers between devices: 6.17 us -> 18.2 us  [body(): lax.all_to_all(sent.reshape(LO * ep_count, rows, wide), ('lo', 'ep'), 0,...]
    all_to_all x1, blocking collectives: 63.3 us -> 57.6 us  [body(): lax.all_to_all(mixed.reshape(hi_count, feat, tok_count), 'hi', 0, 0, tile...]
    unnamed x17 -> x16, local copies, waits for them, and re-layouts: 5.25 us -> 4.42 us
  transfers between devices with their start and end apart: 1 -> 2, of which waited for: 1 -> 2; matrix products, arithmetic and copies ran while one was open for 4% -> 5% of each run, Pallas kernels for 0% -> 0%
where the time goes in v1:
time: 210 us; the launch traced here: 209 us
  blocking collectives  81.9 us (39%)
  starting transfers between devices  60.4 us (29%)
  waiting for transfers between devices  47.3 us (23%)
  local copies, waits for them, and re-layouts  13.6 us (6%)
  matrix products  3.21 us (2%)
  other arithmetic  2.36 us (1%)
    all_to_all x1, blocking collectives, body(): lax.all_to_all(mixed.reshape(hi_count, feat, tok_count), 'hi', 0, 0, tile...  57.6 us
    all_to_all x1, starting transfers between devices, body(): lax.all_to_all(jnp.stack(lax.psum(1, 'hi') * [tokens.T]), 'hi', 0, 0)  42.2 us
    all_to_all x1, waiting for transfers between devices, body(): lax.all_to_all(jnp.stack(lax.psum(1, 'hi') * [tokens.T]), 'hi', 0, 0)  33 us
    all_to_all x1, blocking collectives, body(): lax.all_to_all(part.reshape(LO * ep_count, rows, wide), ('lo', 'ep'), 0,...  24.2 us
    all_to_all x1, starting transfers between devices, body(): lax.all_to_all(sent.reshape(LO * ep_count, rows, wide), ('lo', 'ep'), 0,...  18.2 us
    all_to_all x1, waiting for transfers between devices, body(): lax.all_to_all(sent.reshape(LO * ep_count, rows, wide), ('lo', 'ep'), 0,...  14.4 us
    unnamed x16, local copies, waits for them, and re-layouts  4.42 us
  transfers between devices with their start and end apart: 2, of which 2 were waited for; matrix products, arithmetic and copies ran while one was open for 5% of the time, Pallas kernels for 0%

profile of v1, /device:TPU:166, one launch (start us, length us, event | category | flops | bytes accessed | tf_op | source)
XLA Modules:
  0.0 209.0 jit_solution(2862732457851859951)
XLA Ops:
  0.0 0.8 copy.32
  0.8 0.8 stack.8
  1.6 42.2 %all-to-all-start = ((bf16[16,96,96]{2,1,0:T(8,128)(2,1)}), bf16[16,96,96]{2,1,0:T(8,128)(2,1)S(1)}, u32[]{:S(2)}, u32[]{:S(2)}) async-start(bf16[16,96,96]{2,1,0:T(8,128)(2,1)} %stack.8), calls=%async_computation | async-start | bytes 786432 | tf_op jit(solution)/shard_map/all_to_all | solution.py:39
  43.9 0.8 copy.30
  44.8 0.2 fusion.4
  45.2 0.7 multiply_add_fusion
  45.9 0.8 select_reduce_fusion
  46.7 33.0 %all-to-all-done = bf16[16,96,96]{2,1,0:T(8,128)(2,1)S(1)} async-done(((bf16[16,96,96]{2,1,0:T(8,128)(2,1)}), bf16[16,96,96]{2,1,0:T(8,128)(2,1)S(1)}, u32[]{:S(2)}, u32[]{:S(2)}) %all-to-all-start) | async-done | bytes 294944 | tf_op jit(solution)/shard_map/all_to_all | solution.py:39
  79.7 0.4 convolution_convert_fusion.2
  80.1 1.3 broadcast_in_dim.25
  81.4 18.2 %all-to-all-start.1 = ((bf16[16,32,1536]{2,1,0:T(8,128)(2,1)}), bf16[16,32,1536]{2,1,0:T(8,128)(2,1)S(1)}, u32[]{:S(2)}, u32[]{:S(2)}) async-start(bf16[16,32,1536]{2,1,0:T(8,128)(2,1)} %bitcast.3), calls=%async_computation.1 | async-start | bytes 3145728 | tf_op jit(solution)/shard_map/all_to_all | solution.py:46
  99.6 1.7 copy.33
  101.3 2.7 %fusion.13 = (bf16[1,16,96,256]{3,2,0,1:T(8,128)(2,1)}, bf16[1,16,96,256]{3,2,0,1:T(8,128)(2,1)}) fusion(bf16[2,16,96,256]{3,2,0,1:T(8,128)(2,1)} %bitcast.58), kind=kLoop, calls=%fused_computation.27 | loop fusion | bytes 3145728 | tf_op jit(solution)/shard_map/slice | solution.py:58
  104.1 1.3 fusion.14
  105.4 1.3 fusion.12
  106.7 14.4 %all-to-all-done.1 = bf16[16,32,1536]{2,1,0:T(8,128)(2,1)S(1)} async-done(((bf16[16,32,1536]{2,1,0:T(8,128)(2,1)}), bf16[16,32,1536]{2,1,0:T(8,128)(2,1)S(1)}, u32[]{:S(2)}, u32[]{:S(2)}) %all-to-all-start.1) | async-done | bytes 1572896 | tf_op jit(solution)/shard_map/all_to_all | solution.py:46
  121.2 0.4 fusion.16
  121.5 0.7 copy-done.1
  122.3 0.4 fusion.17
  122.7 0.4 convolution_add_fusion.1
  123.1 0.4 copy-done.6
  123.5 0.4 fusion.3
  123.9 0.4 copy-done.3
  124.2 0.4 fusion
  124.6 0.4 copy-done.2
  125.0 0.4 fusion.1
  125.4 0.1 pad_maximum_fusion
  125.6 24.2 %all_to_all.20 = bf16[16,32,1536]{2,1,0:T(8,128)(2,1)S(1)} all-to-all(bf16[16,32,1536]{2,1,0:T(8,128)(2,1)S(1)} %bitcast.48), channel_id=1, replica_groups=mesh['rep'=2,'hi'=16,'lo'=2,'ep'=8] {'lo','ep'}, dimensions={0} | all-to-all | bytes 3145728 | tf_op jit(solution)/shard_map/all_to_all | solution.py:69
  149.9 0.4 convolution_convert_fusion.3
  150.2 0.3 reshape.66
  150.7 57.6 %all_to_all.21 = bf16[16,96,96]{1,2,0:T(8,128)(2,1)S(1)} all-to-all(bf16[16,96,96]{1,2,0:T(8,128)(2,1)S(1)} %copy.34), channel_id=1, replica_groups=mesh['rep'=2,'hi'=16,'lo'=2,'ep'=8] {'hi'}, dimensions={0} | all-to-all | bytes 589824 | tf_op jit(solution)/shard_map/all_to_all | solution.py:76
  208.3 0.7 reduce_sum.42
  (16 shorter events, 0.6 us)
Async XLA Ops:
  1.6 78.0 %all-to-all-start = ((bf16[16,96,96]{2,1,0:T(8,128)(2,1)}), bf16[16,96,96]{2,1,0:T(8,128)(2,1)S(1)}, u32[]{:S(2)}, u32[]{:S(2)}) async-start(bf16[16,96,96]{2,1,0:T(8,128)(2,1)} %stack.8), calls=%async_computation | async-start | bytes 786432 | tf_op jit(solution)/shard_map/all_to_all | solution.py:39
  81.4 39.7 %all-to-all-start.1 = ((bf16[16,32,1536]{2,1,0:T(8,128)(2,1)}), bf16[16,32,1536]{2,1,0:T(8,128)(2,1)S(1)}, u32[]{:S(2)}, u32[]{:S(2)}) async-start(bf16[16,32,1536]{2,1,0:T(8,128)(2,1)} %bitcast.3), calls=%async_computation.1 | async-start | bytes 3145728 | tf_op jit(solution)/shard_map/all_to_all | solution.py:46
  101.3 2.8 %copy-start.5 = (bf16[1,3072,256]{2,1,0:T(8,128)(2,1)S(1)}, bf16[1,3072,256]{2,1,0:T(8,128)(2,1)}, u32[]{:S(2)}) copy-start(bf16[1,3072,256]{2,1,0:T(8,128)(2,1)} %param.10) | copy-start | bytes 4718596
  106.6 14.5 %copy-start = (bf16[1,16,96,256]{3,2,0,1:T(8,128)(2,1)S(1)}, bf16[1,16,96,256]{3,2,0,1:T(8,128)(2,1)}, u32[]{:S(2)}) copy-start(bf16[1,16,96,256]{3,2,0,1:T(8,128)(2,1)} %get-tuple-element.10) | copy-start | bytes 2359300
  121.1 1.1 copy-start.1
  121.2 1.5 copy-start.4
  122.3 1.2 copy-start.6
  123.0 1.2 copy-start.3
  123.8 1.2 copy-start.2
